TPU v7x, 256 devices: a whole 4x4x8 slice. The times are simulated.
256 devices in a mesh: dp: 64 (over x, z_lo, y, core), mp: 4 (over z_hi).
Axes of the slice: x: 4, y: 4, z: 8 (z_hi: 4, z_lo: 2; z = z_hi * 2 + z_lo), core: 2. Of those that a mesh axis runs over, the one named last changes fastest.
Arguments:
- pooled: bfloat16 [16384, 3584], P('dp', 'mp'), may hold values from -4 to 4
- w_out: bfloat16 [3584, 3584], P('mp'), may hold values from -0.028931878 to 0.028931878
- assignments: int32 [16384], P('dp'), may hold values from 0 to 4095
- ema_sums: float32 [4096, 3584], P('mp', 'dp'), may hold values from -0.40089186 to 0.40089186
- ema_counts: float32 [4096], P('mp'), may hold values from 1 to 8
Outputs:
- distances: float32 [16384, 4096], P('dp', 'mp')
- new_sums: float32 [4096, 3584], P('mp', 'dp')
- new_counts: float32 [4096], P('mp')
- new_centroids: bfloat16 [4096, 3584], P('mp', 'dp')
All inputs are finite; a program needn't handle non-finite values.
Results may differ from a plain program's by a relative error of at most 0.0011.
Values may be sent and summed in bfloat16 or wider, within the bound.
No kernel may reach another device: no remote copies, remote signals or barrier semaphores. Data moves between devices by JAX's collectives and lax.ppermute only.
A program may use at most 64 MiB of HBM per device.

v0:
```python
import math
import jax
import jax.numpy as jnp
from jax import lax
from jax.sharding import PartitionSpec as P

EPSILON = 1e-06
EMA_DECAY = 0.9


def copy_for_each(value, axis):
    copies = jnp.broadcast_to(value, (lax.axis_size(axis), *value.shape))
    return lax.all_to_all(copies, axis, split_axis=0, concat_axis=0, tiled=True)


def over_copies(value, axis):
    everything = copy_for_each(value, axis)
    return jnp.sum(everything, axis=0)


def laid_out(pieces, dim):
    lengths = list(pieces.shape[1:])
    lengths[dim] *= pieces.shape[0]
    return jnp.moveaxis(pieces, 0, dim).reshape(lengths)


def collect(value, axis, dim):
    pieces = copy_for_each(value, axis)
    return laid_out(pieces, dim)


def body(pooled, w_out, assignments, ema_sums, ema_counts):
    partial_value = jnp.dot(pooled, w_out, preferred_element_type=jnp.float32)
    share_part = lax.psum_scatter(partial_value, "mp", scatter_dimension=1, tiled=True)
    squares = over_copies(jnp.sum(share_part * share_part, axis=1), "mp")
    inverse_norm = 1.0 / jnp.sqrt(squares + EPSILON)
    share_embedded = (share_part * inverse_norm[:, None]).astype(jnp.bfloat16)
    embedded = collect(share_embedded, "mp", 1)
    local_centers = ema_sums.shape[0]
    doc_rows = embedded.shape[0]
    centers = (ema_sums / ema_counts[:, None]).astype(jnp.bfloat16)
    column_piece = lax.all_gather(centers, "dp", axis=1, tiled=True)
    products = lax.dot_general(
        embedded, column_piece, (((1,), (1,)), ((), ())), preferred_element_type=jnp.float32
    )
    piece_wide = column_piece.astype(jnp.float32)
    center_norms = jnp.sum(piece_wide * piece_wide, axis=1)
    products, center_norms = (products, center_norms)
    embed_wide = embedded.astype(jnp.float32)
    doc_norms = jnp.sum(embed_wide * embed_wide, axis=1)
    distances = doc_norms[:, None] + center_norms[None, :] - 2.0 * products
    first_center = lax.axis_index("mp") * local_centers
    center_ids = first_center + jnp.arange(local_centers, dtype=jnp.int32)
    feature_cols = ema_sums.shape[1]
    every_assign = collect(assignments, "dp", 0)
    own_columns = lax.all_to_all(embedded, "dp", split_axis=1, concat_axis=0, tiled=True)
    shard_count = lax.axis_size("dp")
    group_size = math.gcd(shard_count, max(1, 2048 // doc_rows))
    block_rows = group_size * doc_rows
    turns = shard_count // group_size

    def add_block(block_index, totals):
        sums_now, counts_now = totals
        block_assign = lax.dynamic_slice_in_dim(
            every_assign, block_index * block_rows, block_rows, 0
        )
        block_columns = lax.dynamic_slice_in_dim(
            own_columns, block_index * block_rows, block_rows, 0
        )
        one_hot = (block_assign[None, :] == center_ids[:, None]).astype(jnp.bfloat16)
        sums_now = sums_now + jnp.dot(one_hot, block_columns, preferred_element_type=jnp.float32)
        counts_now = counts_now + jnp.sum(one_hot, axis=1, dtype=jnp.float32)
        return (sums_now, counts_now)

    start_sums = (
        jnp.zeros((local_centers, feature_cols), jnp.float32),
        jnp.zeros((local_centers,), jnp.float32),
    )
    batch_sums, batch_counts = lax.fori_loop(0, turns, add_block, start_sums)
    new_counts = EMA_DECAY * ema_counts + (1.0 - EMA_DECAY) * batch_counts
    new_sums = EMA_DECAY * ema_sums + (1.0 - EMA_DECAY) * batch_sums
    new_centroids = (new_sums / new_counts[:, None]).astype(jnp.bfloat16)
    return (distances, new_sums, new_counts, new_centroids)


def solution(mesh):
    return jax.shard_map(
        body,
        mesh=mesh,
        in_specs=(P("dp", "mp"), P("mp", None), P("dp"), P("mp", "dp"), P("mp")),
        out_specs=(P("dp", "mp"), P("mp", "dp"), P("mp"), P("mp", "dp")),
        check_vma=False,
    )
```

profile of v0, /device:TPU:1, one launch (start us, length us, event | category | flops | bytes accessed | tf_op | source)
XLA Modules:
  0.0 354.5 jit_solution(18194676151146856325)
XLA Ops:
  7.2 0.0 copy-start
  7.2 0.0 reduce-scatter.2.cloned.1.call-start
  7.2 1.0 copy-done
  8.2 6.7 %fusion.12 = f32[256,3584]{1,0:T(8,128)} fusion(bf16[256,896]{1,0:T(8,128)(2,1)S(1)} %copy-done, bf16[896,3584]{1,0:T(8,128)(2,1)} %param.8), kind=kOutput, calls=%fused_computation.23 | convolution fusion | flops 1644167168 | bytes 10551296 | tf_op jit(solution)/shard_map/dot_general | solution.py:33
  14.9 0.0 reduce-scatter.2.cloned.1.call-update
  14.9 78.5 %reduce-scatter.2.cloned.1.call-done = f32[256,896]{1,0:T(8,128)} async-done(((f32[256,3584]{1,0:T(8,128)}), f32[256,896]{1,0:T(8,128)}) %reduce-scatter.2.cloned.1.call-update) | async-done | bytes 917520 | tf_op jit(solution)/shard_map/reduce_scatter | solution.py:34
  93.4 1.3 multiply_reduce_fusion.2
  94.7 11.3 %all_to_all.36 = f32[4,1,256]{2,1,0:T(1,128)S(1)} all-to-all(f32[4,1,256]{2,1,0:T(1,128)S(1)} %broadcast_in_dim.26), channel_id=1, replica_groups=mesh['dp'=64,'mp'=4] {'mp'}, dimensions={0} | all-to-all | bytes 8192 | tf_op jit(solution)/shard_map/all_to_all | solution.py:13
  106.1 1.3 multiply_convert_fusion
  107.4 0.2 copy.17
  107.6 0.1 broadcast_in_dim.27
  107.7 0.0 copy-start.5
  107.7 41.2 %all_to_all.37 = bf16[4,256,896]{1,2,0:T(8,128)(2,1)S(1)} all-to-all(bf16[4,256,896]{1,2,0:T(8,128)(2,1)S(1)} %broadcast_in_dim.27), channel_id=1, replica_groups=mesh['dp'=64,'mp'=4] {'mp'}, dimensions={0} | all-to-all | bytes 3670016 | tf_op jit(solution)/shard_map/all_to_all | solution.py:13
  148.9 40.8 %all_to_all.38 = bf16[256,64,56]{0,2,1:T(8,128)(2,1)} all-to-all(bf16[256,64,56]{0,2,1:T(8,128)(2,1)S(1)} %bitcast.13), channel_id=1, replica_groups=mesh['dp'=64,'mp'=4] {'dp'}, dimensions={1} | all-to-all | bytes 3670016 | tf_op jit(solution)/shard_map/all_to_all | solution.py:56
  189.7 0.0 copy-done.5
  189.7 0.7 broadcast_in_dim.30
  190.4 4.7 %all-to-all-start.2 = ((s32[64,1,256]{2,1,0:T(1,128)}), s32[64,1,256]{2,1,0:T(1,128)S(1)}, u32[]{:S(2)}, u32[]{:S(2)}) async-start(s32[64,1,256]{2,1,0:T(1,128)} %broadcast_in_dim.30), calls=%async_computation.3 | async-start | bytes 131072 | tf_op jit(solution)/shard_map/all_to_all | solution.py:13
  195.1 0.0 all-gather.2.cloned.1.call-start
  195.2 4.7 %copy.20 = bf16[64,256,56]{2,1,0:T(8,128)(2,1)} copy(bf16[64,256,56]{1,2,0:T(8,128)(2,1)} %bitcast.15) | data formatting | bytes 3670016
  199.9 3.3 all-to-all-done.2
  203.2 0.0 copy-start.3
  203.2 0.0 copy-start.2
  203.2 28.9 %while.16 = (s32[]{:T(128)}, f32[1024,56]{0,1:T(8,128)S(1)}, f32[1024]{0:T(1024)S(1)}, s32[16384]{0:T(1024)S(1)}, bf16[16384,56]{1,0:T(8,128)(2,1)}, /*index=5*/...) while((s32[]{:T(128)}, f32[1024,56]{0,1:T(8,128)S(1)}, f32[1024]{0:T(1024)S(1)}, ...), condition=%wide.region_7.0_spmd.clone, body=%wide.region_5.0_spmd.clone.sunk | while | flops 245483520 | bytes 1044658 | solution.py:79
  203.3 1.0 convert_reduce_fusion.2
  204.2 2.6 fusion.22
  206.9 1.0 convert_reduce_fusion.2
  207.8 2.6 fusion.22
  210.5 1.0 convert_reduce_fusion.2
  211.5 2.6 fusion.22
  214.1 1.0 convert_reduce_fusion.2
  215.1 2.6 fusion.22
  217.7 1.0 convert_reduce_fusion.2
  218.7 2.6 fusion.22
  221.3 1.0 convert_reduce_fusion.2
  222.3 2.6 fusion.22
  225.0 1.0 convert_reduce_fusion.2
  225.9 2.6 fusion.22
  228.6 1.0 convert_reduce_fusion.2
  229.5 2.6 fusion.22
  232.2 0.0 copy-done.3
  232.2 0.0 copy-start.4
  232.2 0.0 copy-done.2
  232.2 0.8 divide_convert_fusion
  233.0 0.0 all-gather.2.cloned.1.call-update
  233.1 0.5 multiply_reduce_fusion.1
  233.6 105.9 %all-gather.2.cloned.1.call-done = bf16[1024,3584]{0,1:T(8,128)(2,1)} async-done(((bf16[1024,56]{0,1:T(8,128)(2,1)}), bf16[1024,3584]{0,1:T(8,128)(2,1)}) %all-gather.2.cloned.1.call-update) | async-done | bytes 7340048 | tf_op jit(solution)/shard_map/all_gather | solution.py:42
  339.5 0.0 copy-start.1
  339.5 4.7 %multiply_reduce_fusion = f32[1024]{0:T(1024)S(1)} fusion(bf16[1024,3584]{0,1:T(8,128)(2,1)} %all-gather.2.cloned.1.call-done), kind=kLoop, calls=%fused_computation.12 | loop fusion | flops 11009024 | bytes 7344128 | tf_op jit(solution)/shard_map/reduce_sum | solution.py:47
  344.2 0.0 copy-done.4
  344.2 0.4 copy-done.1
  344.6 3.1 fusion.11
  (30 shorter events, 0.2 us)
Async XLA Ops:
  7.2 1.0 copy-start
  7.2 86.2 %reduce-scatter.2.cloned.1.call-start = ((), (), s32[]{:S(2)}) async-start(), calls=%async_computation.5 | async-start | bytes 4587520 | tf_op jit(solution)/shard_map/reduce_scatter | solution.py:34
  107.7 82.0 %copy-start.5 = (s32[256]{0:T(256)S(1)}, s32[256]{0:T(256)}, u32[]{:S(2)}) copy-start(s32[256]{0:T(256)} %param.9) | copy-start | bytes 3076
  190.4 12.8 %all-to-all-start.2 = ((s32[64,1,256]{2,1,0:T(1,128)}), s32[64,1,256]{2,1,0:T(1,128)S(1)}, u32[]{:S(2)}, u32[]{:S(2)}) async-start(s32[64,1,256]{2,1,0:T(1,128)} %broadcast_in_dim.30), calls=%async_computation.3 | async-start | bytes 131072 | tf_op jit(solution)/shard_map/all_to_all | solution.py:13
  195.1 144.3 %all-gather.2.cloned.1.call-start = ((), (), s32[]{:S(2)}) async-start(), calls=%async_computation.6 | async-start | bytes 7454720 | tf_op jit(solution)/shard_map/all_gather | solution.py:42
  203.2 28.9 %copy-start.3 = (f32[1024]{0:T(1024)S(1)}, f32[1024]{0:T(1024)}, u32[]{:S(2)}) copy-start(f32[1024]{0:T(1024)} %param.11) | copy-start | bytes 12292
  203.2 29.0 %copy-start.2 = (f32[1024,56]{0,1:T(8,128)S(1)}, f32[1024,56]{0,1:T(8,128)}, u32[]{:S(2)}) copy-start(f32[1024,56]{0,1:T(8,128)} %param.10) | copy-start | bytes 688132
  232.2 112.0 %copy-start.4 = (f32[1024]{0:T(1024)}, f32[1024]{0:T(1024)S(1)}, u32[]{:S(2)}) copy-start(f32[1024]{0:T(1024)S(1)} %multiply_add_fusion.1) | copy-start | bytes 12292
  339.5 5.2 %copy-start.1 = (bf16[1024,3584]{0,1:T(8,128)(2,1)S(1)}, bf16[1024,3584]{0,1:T(8,128)(2,1)}, u32[]{:S(2)}) copy-start(bf16[1024,3584]{0,1:T(8,128)(2,1)} %all-gather.2.cloned.1.call-done) | copy-start | bytes 22020100
Sparse Core Ops, SparseCore 0:
  15.0 78.3 reduce-scatter.1
  233.2 106.2 all-gather.1
where the time goes:
time: 355 us
  waiting for transfers between devices  188 us (53%)
  blocking collectives  93.3 us (26%)
  matrix products  30.5 us (9%)
  other arithmetic  16.4 us (5%)
  between operations  14.2 us (4%)
  local copies, waits for them, and re-layouts  7.24 us (2%)
  starting transfers between devices  4.83 us (1%)
    all_gather x1, waiting for transfers between devices, body(): column_piece = lax.all_gather(centers, 'dp', axis=1, tiled=True)  106 us
    reduce_scatter x1, waiting for transfers between devices, body(): lax.psum_scatter(partial_value, 'mp', scatter_dimension=1, tiled=True)  78.5 us
    all_to_all x2, blocking collectives, copy_for_each(): return lax.all_to_all(copies, axis, split_axis=0, concat_axis=0, tiled=True)  52.5 us
    all_to_all x1, blocking collectives, body(): lax.all_to_all(embedded, 'dp', split_axis=1, concat_axis=0, tiled=True)  40.8 us
    dot_general x8, matrix products, add_block(): jnp.dot(one_hot, block_columns, preferred_element_type=jnp.float32)  20.7 us
    reduce_sum x8, other arithmetic, add_block(): counts_now = counts_now + jnp.sum(one_hot, axis=1, dtype=jnp.float32)  7.61 us
  transfers between devices with their start and end apart: 3, of which 3 were waited for; matrix products, arithmetic and copies ran while one was open for 1% of the time, Pallas kernels for 0%

commit v1 on v0

--- a/solution.py
+++ b/solution.py
@@ -39,7 +39,7 @@
     local_centers = ema_sums.shape[0]
     doc_rows = embedded.shape[0]
     centers = (ema_sums / ema_counts[:, None]).astype(jnp.bfloat16)
-    column_piece = lax.all_gather(centers, "dp", axis=1, tiled=True)
+    column_piece = jnp.concatenate(lax.all_gather(centers, "dp"), axis=1)
     products = lax.dot_general(
         embedded, column_piece, (((1,), (1,)), ((), ())), preferred_element_type=jnp.float32
     )

time: 355 us -> 370 us (1.042)
  local copies, waits for them, and re-layouts: 7.24 us -> 21.3 us
    reshape x0 -> x1, local copies, waits for them, and re-layouts: none -> 7.09 us  [body(): column_piece = jnp.concatenate(lax.all_gather(centers, 'dp'), axis=1)]
    unnamed x13 -> x12, local copies, waits for them, and re-layouts: 6.15 us -> 13.2 us
where the time goes in v1:
time: 370 us; the launch traced here: 369 us
  waiting for transfers between devices  188 us (51%)
  blocking collectives  93.3 us (25%)
  matrix products  33.6 us (9%)
  local copies, waits for them, and re-layouts  21.3 us (6%)
  between operations  14.2 us (4%)
  other arithmetic  13.7 us (4%)
  starting transfers between devices  4.83 us (1%)
    all_gather x1, waiting for transfers between devices, body(): column_piece = jnp.concatenate(lax.all_gather(centers, 'dp'), axis=1)  106 us
    reduce_scatter x1, waiting for transfers between devices, body(): lax.psum_scatter(partial_value, 'mp', scatter_dimension=1, tiled=True)  78.5 us
    all_to_all x2, blocking collectives, copy_for_each(): return lax.all_to_all(copies, axis, split_axis=0, concat_axis=0, tiled=True)  55.6 us
    all_to_all x1, blocking collectives, body(): lax.all_to_all(embedded, 'dp', split_axis=1, concat_axis=0, tiled=True)  37.7 us
    dot_general x8, matrix products, add_block(): jnp.dot(one_hot, block_columns, preferred_element_type=jnp.float32)  20.8 us
    unnamed x12, local copies, waits for them, and re-layouts  13.2 us
    reduce_sum x8, other arithmetic, add_block(): counts_now = counts_now + jnp.sum(one_hot, axis=1, dtype=jnp.float32)  7.6 us
  transfers between devices with their start and end apart: 3, of which 3 were waited for; matrix products, arithmetic and copies ran while one was open for 1% of the time, Pallas kernels for 0%

profile of v1, /device:TPU:1, one launch (start us, length us, event | category | flops | bytes accessed | tf_op | source)
XLA Modules:
  0.0 369.3 jit_solution(9500113627075388973)
XLA Ops:
  7.2 0.0 copy-start
  7.2 0.0 reduce-scatter.2.cloned.1.call-start
  7.2 1.0 copy-done
  8.2 6.7 %fusion.12 = f32[256,3584]{1,0:T(8,128)} fusion(bf16[256,896]{1,0:T(8,128)(2,1)S(1)} %copy-done, bf16[896,3584]{1,0:T(8,128)(2,1)} %param.8), kind=kOutput, calls=%fused_computation.23 | convolution fusion | flops 1644167168 | bytes 10551296 | tf_op jit(solution)/shard_map/dot_general | solution.py:33
  14.9 0.0 reduce-scatter.2.cloned.1.call-update
  14.9 0.0 copy-start.4
  14.9 78.5 %reduce-scatter.2.cloned.1.call-done = f32[256,896]{1,0:T(8,128)} async-done(((f32[256,3584]{1,0:T(8,128)}), f32[256,896]{1,0:T(8,128)}) %reduce-scatter.2.cloned.1.call-update) | async-done | bytes 917520 | tf_op jit(solution)/shard_map/reduce_scatter | solution.py:34
  93.4 1.3 multiply_reduce_fusion.2
  94.7 11.3 %all_to_all.36 = f32[4,1,256]{2,1,0:T(1,128)S(1)} all-to-all(f32[4,1,256]{2,1,0:T(1,128)S(1)} %broadcast_in_dim.26), channel_id=1, replica_groups=mesh['dp'=64,'mp'=4] {'mp'}, dimensions={0} | all-to-all | bytes 8192 | tf_op jit(solution)/shard_map/all_to_all | solution.py:13
  106.1 1.3 multiply_convert_fusion
  107.4 0.2 copy.19
  107.6 0.1 broadcast_in_dim.27
  107.7 44.3 %all_to_all.37 = bf16[4,256,896]{1,2,0:T(8,128)(2,1)S(1)} all-to-all(bf16[4,256,896]{1,2,0:T(8,128)(2,1)S(1)} %broadcast_in_dim.27), channel_id=1, replica_groups=mesh['dp'=64,'mp'=4] {'mp'}, dimensions={0} | all-to-all | bytes 3670016 | tf_op jit(solution)/shard_map/all_to_all | solution.py:13
  152.0 37.7 %all_to_all.38 = bf16[256,64,56]{0,2,1:T(8,128)(2,1)} all-to-all(bf16[256,64,56]{0,2,1:T(8,128)(2,1)S(1)} %bitcast.24), channel_id=1, replica_groups=mesh['dp'=64,'mp'=4] {'dp'}, dimensions={1} | all-to-all | bytes 3670016 | tf_op jit(solution)/shard_map/all_to_all | solution.py:56
  189.7 0.0 copy-done.4
  189.7 0.7 broadcast_in_dim.30
  190.4 4.7 %all-to-all-start.2 = ((s32[64,1,256]{2,1,0:T(1,128)}), s32[64,1,256]{2,1,0:T(1,128)S(1)}, u32[]{:S(2)}, u32[]{:S(2)}) async-start(s32[64,1,256]{2,1,0:T(1,128)} %broadcast_in_dim.30), calls=%async_computation.3 | async-start | bytes 131072 | tf_op jit(solution)/shard_map/all_to_all | solution.py:13
  195.1 0.0 all-gather.3.cloned.1.call-start
  195.2 4.7 %copy.23 = bf16[64,256,56]{2,1,0:T(8,128)(2,1)} copy(bf16[64,256,56]{1,2,0:T(8,128)(2,1)} %bitcast.27) | data formatting | bytes 3670016
  199.9 3.3 all-to-all-done.2
  203.2 0.0 copy-start.2
  203.2 0.0 copy-start.1
  203.2 29.1 %while.16 = (s32[]{:T(128)}, f32[1024,56]{0,1:T(8,128)S(1)}, f32[1024]{0:T(1024)S(1)}, s32[16384]{0:T(1024)S(1)}, bf16[16384,56]{1,0:T(8,128)(2,1)}, /*index=5*/...) while((s32[]{:T(128)}, f32[1024,56]{0,1:T(8,128)S(1)}, f32[1024]{0:T(1024)S(1)}, ...), condition=%wide.region_7.0_spmd.clone, body=%wide.region_5.0_spmd.clone.sunk | while | flops 245483520 | bytes 1044650 | solution.py:79
  203.2 2.6 fusion.22
  205.9 1.0 convert_reduce_fusion.2
  206.9 2.6 fusion.22
  209.5 1.0 convert_reduce_fusion.2
  210.5 2.6 fusion.22
  213.1 1.0 convert_reduce_fusion.2
  214.1 2.6 fusion.22
  216.7 1.0 convert_reduce_fusion.2
  217.8 2.6 fusion.22
  220.4 1.0 convert_reduce_fusion.2
  221.4 2.6 fusion.22
  224.0 1.0 convert_reduce_fusion.2
  225.0 2.6 fusion.22
  227.6 1.0 convert_reduce_fusion.2
  228.6 2.6 fusion.22
  231.2 1.0 convert_reduce_fusion.2
  232.4 0.0 copy-done.2
  232.4 0.0 copy-start.3
  232.4 0.0 copy-done.1
  232.4 0.8 divide_convert_fusion
  233.3 0.0 all-gather.3.cloned.1.call-update
  233.3 0.5 multiply_reduce_fusion.1
  233.8 106.0 %all-gather.3.cloned.1.call-done = bf16[65536,56]{0,1:T(8,128)(2,1)} async-done(((bf16[1024,56]{0,1:T(8,128)(2,1)}), bf16[65536,56]{0,1:T(8,128)(2,1)}) %all-gather.3.cloned.1.call-update) | async-done | bytes 7340048 | tf_op jit(solution)/shard_map/all_gather | solution.py:42
  339.8 7.4 %copy.26 = bf16[7,8,64,1024]{3,2,1,0:T(8,128)(2,1)S(1)} copy(bf16[7,8,64,1024]{3,1,2,0:T(8,128)(2,1)} %bitcast.26) | data formatting | bytes 14680064
  347.2 0.0 copy-done.3
  347.2 2.0 multiply_reduce_fusion
  349.2 7.1 %copy.20 = bf16[1024,64,56]{0,2,1:T(8,128)(2,1)} copy(bf16[1024,64,56]{0,1,2:T(8,128)(2,1)S(1)} %bitcast.22) | data formatting | bytes 14680064 | tf_op jit(solution)/shard_map/reshape | solution.py:42
  356.3 6.1 %fusion.11 = f32[256,1024]{1,0:T(8,128)} fusion(bf16[256,3584]{0,1:T(8,128)(2,1)S(1)} %bitcast.25, bf16[1024,3584]{0,1:T(8,128)(2,1)} %bitcast.23, f32[1024]{0:T(1024)S(1)} %multiply_reduce_fusion, f32[256]{0:T(256)S(1)} %multiply_reduce_fusion.1), kind=kOutput, calls=%fused_computation.15 | convolution fusion | flops 1879834624 | bytes 10228736 | tf_op jit(solution)/shard_map/dot_general | solution.py:43
  (30 shorter events, 0.2 us)
Async XLA Ops:
  7.2 1.0 copy-start
  7.2 86.2 %reduce-scatter.2.cloned.1.call-start = ((), (), s32[]{:S(2)}) async-start(), calls=%async_computation.5 | async-start | bytes 4587520 | tf_op jit(solution)/shard_map/reduce_scatter | solution.py:34
  14.9 174.8 %copy-start.4 = (s32[256]{0:T(256)S(1)}, s32[256]{0:T(256)}, u32[]{:S(2)}) copy-start(s32[256]{0:T(256)} %param.9) | copy-start | bytes 3076
  190.4 12.8 %all-to-all-start.2 = ((s32[64,1,256]{2,1,0:T(1,128)}), s32[64,1,256]{2,1,0:T(1,128)S(1)}, u32[]{:S(2)}, u32[]{:S(2)}) async-start(s32[64,1,256]{2,1,0:T(1,128)} %broadcast_in_dim.30), calls=%async_computation.3 | async-start | bytes 131072 | tf_op jit(solution)/shard_map/all_to_all | solution.py:13
  195.1 144.6 %all-gather.3.cloned.1.call-start = ((), (), s32[]{:S(2)}) async-start(), calls=%async_computation.6 | async-start | bytes 7454720 | tf_op jit(solution)/shard_map/all_gather | solution.py:42
  203.2 29.2 %copy-start.2 = (f32[1024]{0:T(1024)S(1)}, f32[1024]{0:T(1024)}, u32[]{:S(2)}) copy-start(f32[1024]{0:T(1024)} %param.11) | copy-start | bytes 12292
  203.2 29.2 %copy-start.1 = (f32[1024,56]{0,1:T(8,128)S(1)}, f32[1024,56]{0,1:T(8,128)}, u32[]{:S(2)}) copy-start(f32[1024,56]{0,1:T(8,128)} %param.10) | copy-start | bytes 688132
  232.4 114.8 %copy-start.3 = (f32[1024]{0:T(1024)}, f32[1024]{0:T(1024)S(1)}, u32[]{:S(2)}) copy-start(f32[1024]{0:T(1024)S(1)} %multiply_add_fusion.1) | copy-start | bytes 12292
Sparse Core Ops, SparseCore 0:
  15.0 78.3 reduce-scatter.1
  233.4 106.3 all-gather.2
